TPU v7x, 32 devices: a whole 2x2x4 slice. The times are simulated.
32 devices in a mesh: row: 8 (over z, y), col: 4 (over x, core).
Axes of the slice: x: 2, y: 2, z: 4, core: 2. Of those that a mesh axis runs over, the one named last changes fastest.
Arguments:
- layer_input: bfloat16 [2048, 8192], P('row'), may hold values from -7 to 7
- gain: float32 [8192], replicated, may hold values from 0.5 to 6
- d_query: bfloat16 [2048, 4096], P('row', 'col'), may hold values from -6 to 6
- d_keyval: bfloat16 [2048, 2048], P('row', 'col'), may hold values from -6 to 6
- w_query: bfloat16 [8192, 4096], P('row', 'col'), may hold values from -0.0625 to 0.0625
- w_keyval: bfloat16 [8192, 2048], P('row', 'col'), may hold values from -1 to 1
- d_resid: bfloat16 [2048, 8192], P('row', 'col'), may hold values from -6 to 6
Outputs:
- d_input: bfloat16 [2048, 8192], P('row', 'col')
- grad_wq: bfloat16 [8192, 4096], P('row', 'col')
- grad_wkv: bfloat16 [8192, 2048], P('row', 'col')
- grad_gain: float32 [8192], P('col')
- grad_square_sum: float32 [], replicated
All inputs are finite; a program needn't handle non-finite values.
Results may differ from a plain program's by a relative error of at most 0.023.
Values may be sent and summed in bfloat16 or wider, within the bound.
A program may use at most 128 MiB of HBM per device.

v0:
```python
import math
import jax
import jax.numpy as jnp
from jax import lax
from jax.sharding import PartitionSpec as P

epsilon = 1e-05


def local(layer_input, gain, d_query, d_keyval, w_query, w_keyval, d_resid):
    inputs = layer_input.astype(jnp.float32)
    inv_rms = lax.rsqrt(jnp.mean(inputs * inputs, axis=1, keepdims=True) + epsilon)
    normed = (inputs * inv_rms * gain).astype(jnp.bfloat16)
    model_width = inputs.shape[1]
    local_tokens = inputs.shape[0]
    tokens_all = local_tokens * lax.axis_size("row")
    scaling = 1.0 / math.sqrt(tokens_all)
    weight_scale = 1.0 / math.sqrt(local_tokens)
    contract_cols = (((1,), (1,)), ((), ()))
    query_cols = d_query.shape[1]
    cotangent = jnp.concatenate([d_query, d_keyval], axis=1)
    all_cotangents = lax.all_gather(cotangent, "row", axis=0, tiled=True)
    weights = jnp.concatenate([w_query, w_keyval], axis=1)
    partial_value = lax.dot_general(
        all_cotangents, weights, contract_cols, preferred_element_type=jnp.float32
    )
    reduced = lax.psum_scatter(
        partial_value.astype(jnp.bfloat16), "col", scatter_dimension=0, tiled=True
    )
    n_row, n_col = (lax.axis_size("row"), lax.axis_size("col"))
    fold = n_row // n_col
    pieces = reduced.reshape(fold, local_tokens, reduced.shape[1])
    row, col = (lax.axis_index("row"), lax.axis_index("col"))
    arrived = []
    for shift in range(fold):
        pairs = [
            (r * n_col + c, (fold * c + (r + shift) % fold) * n_col + r // fold)
            for r in range(n_row)
            for c in range(n_col)
        ]
        piece = lax.dynamic_index_in_dim(pieces, (row + shift) % fold, 0, keepdims=False)
        arrived.append(lax.ppermute(piece, ("row", "col"), pairs))
    arrived = jnp.stack(arrived)
    feature_grad = jnp.concatenate(
        [
            lax.dynamic_index_in_dim(arrived, (row - j + fold) % fold, 0, keepdims=False)
            for j in range(fold)
        ],
        axis=1,
    ).astype(jnp.float32)
    slice_width = feature_grad.shape[1]
    col_start = lax.axis_index("col") * slice_width
    input_part = lax.dynamic_slice_in_dim(inputs, col_start, slice_width, 1)
    gain_part = lax.dynamic_slice_in_dim(gain, col_start, slice_width, 0)
    weighted = gain_part * feature_grad
    token_dot = lax.psum(jnp.sum(weighted * input_part, axis=1, keepdims=True), "col")
    d_input = (
        d_resid.astype(jnp.float32)
        + inv_rms * weighted
        - input_part * inv_rms**3 * token_dot / model_width
    ).astype(jnp.bfloat16)
    gain_partial = jnp.sum(feature_grad * input_part * inv_rms, axis=0) * scaling
    cotangent = jnp.concatenate([d_query, d_keyval], axis=1)
    columns = lax.all_to_all(normed, "row", split_axis=1, concat_axis=0, tiled=True)
    groups = lax.axis_size("row")
    column_blocks = columns.reshape(groups, local_tokens, columns.shape[1])
    grad_blocks = all_cotangents.reshape(groups, local_tokens, all_cotangents.shape[1])
    blocks = (
        lax.dot_general(
            column_blocks,
            grad_blocks,
            (((1,), (1,)), ((0,), (0,))),
            preferred_element_type=jnp.float32,
        )
        * weight_scale
    )
    summed = jnp.sum(blocks.astype(jnp.bfloat16).astype(jnp.float32), axis=0)
    grad_wq = summed[:, :query_cols].astype(jnp.bfloat16)
    grad_wkv = summed[:, query_cols:].astype(jnp.bfloat16)
    query_f = grad_wq.astype(jnp.float32)
    keyval_f = grad_wkv.astype(jnp.float32)
    tile_square = jnp.sum(query_f * query_f) + jnp.sum(keyval_f * keyval_f)
    grad_gain = lax.psum(gain_partial, "row")
    leading = jnp.where(
        lax.axis_index("row") == 0, jnp.sum(grad_gain * grad_gain), jnp.float32(0.0)
    )
    grand_total = lax.psum(tile_square + leading, ("row", "col"))
    grad_square_sum = grand_total / jnp.float32(model_width)
    return (d_input, grad_wq, grad_wkv, grad_gain, grad_square_sum)


def solution(mesh):
    placed = (
        P("row", None),
        P(),
        P("row", "col"),
        P("row", "col"),
        P("row", "col"),
        P("row", "col"),
        P("row", "col"),
    )
    return jax.shard_map(
        local,
        mesh=mesh,
        in_specs=placed,
        out_specs=(P("row", "col"), P("row", "col"), P("row", "col"), P("col"), P()),
        check_vma=False,
    )
```

profile of v0, /device:TPU:13, one launch (start us, length us, event | category | flops | bytes accessed | tf_op | source)
XLA Modules:
  0.0 376.0 jit_solution(1316032979656445743)
XLA Ops:
  7.2 0.0 copy-start.2
  7.2 0.0 all-gather.2.cloned.1.call-start
  7.2 2.1 pad_maximum_fusion.1
  9.3 0.0 all-gather.2.cloned.1.call-update
  9.3 0.0 copy-start
  9.3 3.3 multiply_reduce_fusion
  12.6 0.0 copy-done.2
  12.6 0.2 copy-done
  12.8 3.1 multiply_convert_fusion.1
  15.9 6.5 %copy.12 = bf16[256,8192]{0,1:T(8,128)(2,1)} copy(bf16[256,8192]{1,0:T(8,128)(2,1)} %multiply_convert_fusion.1) | data formatting | bytes 8388608 | tf_op jit(solution)/shard_map/convert_element_type | solution.py:13
  22.3 0.0 copy-start.4
  22.3 5.8 %all-to-all-start = ((bf16[256,8,1024]{0,2,1:T(8,128)(2,1)}), bf16[256,8,1024]{0,2,1:T(8,128)(2,1)}, u32[]{:S(2)}, u32[]{:S(2)}) async-start(bf16[256,8,1024]{0,2,1:T(8,128)(2,1)} %bitcast.18), calls=%async_computation.1 | async-start | bytes 8388608 | tf_op jit(solution)/shard_map/all_to_all | solution.py:64
  28.1 0.0 reduce-scatter.2.cloned.1.call-start
  28.1 150.8 %all-gather.2.cloned.1.call-done = bf16[2048,1536]{1,0:T(8,128)(2,1)} async-done(((bf16[256,1536]{1,0:T(8,128)(2,1)}), bf16[2048,1536]{1,0:T(8,128)(2,1)}) %all-gather.2.cloned.1.call-update) | async-done | bytes 6291472 | tf_op jit(solution)/shard_map/all_gather | solution.py:22
  179.0 0.0 copy-done.4
  179.0 10.4 %convolution_convert_fusion = bf16[2048,1024]{1,0:T(8,128)(2,1)} fusion(bf16[2048,1536]{1,0:T(8,128)(2,1)} %all-gather.2.cloned.1.call-done, bf16[1024,512]{1,0:T(8,128)(2,1)} %param.12, bf16[1024,1024]{1,0:T(8,128)(2,1)S(1)} %copy-done.4), kind=kOutput, calls=%fused_computation.6 | convolution fusion | flops 6450839552 | bytes 13631488 | tf_op jit(solution)/shard_map/dot_general | solution.py:24
  189.4 0.0 reduce-scatter.2.cloned.1.call-update
  189.5 6.4 %convert_element_type.33 = f32[256,8192]{1,0:T(8,128)} convert(bf16[256,8192]{1,0:T(8,128)(2,1)} %param.7) | non-fusion elementwise | flops 2097152 | bytes 12582912 | tf_op jit(solution)/shard_map/convert_element_type | solution.py:11
  195.9 0.0 all-to-all-done
  195.9 10.9 %fusion = bf16[1024,1536]{1,0:T(8,128)(2,1)S(1)} fusion(bf16[8,256,1536]{2,1,0:T(8,128)(2,1)} %bitcast.20, bf16[256,8,1024]{0,2,1:T(8,128)(2,1)} %all-to-all-done), kind=kOutput, calls=%fused_computation.3 | convolution fusion | flops 6478626816 | bytes 13631488 | tf_op jit(solution)/shard_map/dot_general | solution.py:69
  206.8 36.0 %reduce-scatter.2.cloned.1.call-done = bf16[512,1024]{1,0:T(8,128)(2,1)} async-done(((bf16[2048,1024]{1,0:T(8,128)(2,1)}), bf16[512,1024]{1,0:T(8,128)(2,1)}) %reduce-scatter.2.cloned.1.call-update) | async-done | bytes 1048592 | tf_op jit(solution)/shard_map/reduce_scatter | solution.py:27
  242.8 2.3 dynamic-slice_bitcast_fusion
  245.1 0.3 collective-permute-start.1
  245.3 5.3 %collective-permute-start = (bf16[256,1024]{1,0:T(8,128)(2,1)}, bf16[256,1024]{1,0:T(8,128)(2,1)}, u32[]{:S(2)}, u32[]{:S(2)}) collective-permute-start(bf16[256,1024]{1,0:T(8,128)(2,1)} %get-tuple-element.14), channel_id=1, source_target_pairs={{0,0},{1,8},{2,16},{3,24},{4,4},{5,12},{6,20},{7,28},{8,1},{9,9},{... | collective-permute-start | bytes 1572872 | tf_op jit(solution)/shard_map/ppermute | solution.py:42
  250.7 2.0 multiply_reduce_fusion.2
  252.7 2.9 multiply_reduce_fusion.1
  255.7 0.0 copy-start.1
  257.1 2.3 collective-permute-done.1
  259.3 0.0 collective-permute-done
  259.3 1.6 fusion.16
  260.9 2.2 fusion.12
  263.2 47.4 %psum.22 = f32[2048]{0:T(1024)S(1)} all-reduce(f32[2048]{0:T(1024)S(1)} %broadcast_multiply_fusion), channel_id=1, replica_groups=mesh['row'=8,'col'=4] {'row'}, use_global_device_ids=true, to_apply=%region_6.7 | all-reduce | flops 2048 | bytes 16384 | tf_op jit(solution)/shard_map/psum | solution.py:83
  310.5 0.0 copy-start.3
  310.5 0.6 multiply_reduce_fusion.3
  311.8 45.0 %psum.23 = f32[]{:T(128)} all-reduce(f32[]{:T(128)S(6)} %add.80), channel_id=1, replica_groups=mesh['row'=8,'col'=4] {'row','col'}, use_global_device_ids=true, to_apply=%region_10.11 | all-reduce | flops 1 | bytes 8 | tf_op jit(solution)/shard_map/psum | solution.py:87
  356.8 7.3 %psum.21 = f32[256]{0:T(256)S(1)} all-reduce(f32[256]{0:T(256)S(1)} %get-tuple-element.6), channel_id=1, replica_groups=mesh['row'=8,'col'=4] {'col'}, use_global_device_ids=true, to_apply=%region_3.4 | all-reduce | flops 256 | bytes 2048 | tf_op jit(solution)/shard_map/psum | solution.py:56
  364.8 0.0 copy-done.1
  364.8 3.3 fusion.9
  368.1 0.0 copy-done.3
  (3 shorter events, 0.0 us)
Async XLA Ops:
  7.2 5.4 %copy-start.2 = (f32[8192]{0:T(1024)S(1)}, f32[8192]{0:T(1024)}, u32[]{:S(2)}) copy-start(f32[8192]{0:T(1024)} %param.8) | copy-start | bytes 98308
  7.2 171.8 %all-gather.2.cloned.1.call-start = ((), (), s32[]{:S(2)}) async-start(), calls=%async_computation.2 | async-start | bytes 7077888 | tf_op jit(solution)/shard_map/all_gather | solution.py:22
  9.3 3.5 copy-start
  22.3 156.6 %copy-start.4 = (bf16[1024,1024]{1,0:T(8,128)(2,1)S(1)}, bf16[1024,1024]{1,0:T(8,128)(2,1)}, u32[]{:S(2)}) copy-start(bf16[1024,1024]{1,0:T(8,128)(2,1)} %param.11) | copy-start | bytes 6291460
  22.3 173.5 %all-to-all-start = ((bf16[256,8,1024]{0,2,1:T(8,128)(2,1)}), bf16[256,8,1024]{0,2,1:T(8,128)(2,1)}, u32[]{:S(2)}, u32[]{:S(2)}) async-start(bf16[256,8,1024]{0,2,1:T(8,128)(2,1)} %bitcast.18), calls=%async_computation.1 | async-start | bytes 8388608 | tf_op jit(solution)/shard_map/all_to_all | solution.py:64
  28.1 214.7 %reduce-scatter.2.cloned.1.call-start = ((), (), s32[]{:S(2)}) async-start(), calls=%async_computation.3 | async-start | bytes 5242880 | tf_op jit(solution)/shard_map/reduce_scatter | solution.py:27
  245.1 14.3 %collective-permute-start.1 = (bf16[256,1024]{1,0:T(8,128)(2,1)}, bf16[256,1024]{1,0:T(8,128)(2,1)}, u32[]{:S(2)}, u32[]{:S(2)}) collective-permute-start(bf16[256,1024]{1,0:T(8,128)(2,1)} %get-tuple-element.13), channel_id=1, source_target_pairs={{0,4},{1,12},{2,20},{3,28},{4,0},{5,8},{6,16},{7,24},{8,5},{9,13},... | collective-permute-start | bytes 1572872 | tf_op jit(solution)/shard_map/ppermute | solution.py:42
  245.3 14.0 %collective-permute-start = (bf16[256,1024]{1,0:T(8,128)(2,1)}, bf16[256,1024]{1,0:T(8,128)(2,1)}, u32[]{:S(2)}, u32[]{:S(2)}) collective-permute-start(bf16[256,1024]{1,0:T(8,128)(2,1)} %get-tuple-element.14), channel_id=1, source_target_pairs={{0,0},{1,8},{2,16},{3,24},{4,4},{5,12},{6,20},{7,28},{8,1},{9,9},{... | collective-permute-start | bytes 1572872 | tf_op jit(solution)/shard_map/ppermute | solution.py:42
  255.7 109.1 %copy-start.1 = (bf16[256,2048]{1,0:T(8,128)(2,1)S(1)}, bf16[256,2048]{1,0:T(8,128)(2,1)}, u32[]{:S(2)}) copy-start(bf16[256,2048]{1,0:T(8,128)(2,1)} %param.13) | copy-start | bytes 3145732
  310.5 57.5 %copy-start.3 = (f32[2048]{0:T(1024)}, f32[2048]{0:T(1024)S(1)}, u32[]{:S(2)}) copy-start(f32[2048]{0:T(1024)S(1)} %psum.22) | copy-start | bytes 24580
Sparse Core Ops, SparseCore 0:
  10.7 168.1 all-gather.1
  189.5 53.2 reduce-scatter.1
where the time goes:
time: 377 us; the launch traced here: 376 us
  waiting for transfers between devices  189 us (50%)
  blocking collectives  99.7 us (26%)
  other arithmetic  27.5 us (7%)
  matrix products  21.3 us (6%)
  between operations  18 us (5%)
  starting transfers between devices  11.4 us (3%)
  local copies, waits for them, and re-layouts  8.96 us (2%)
    all_gather x1, waiting for transfers between devices, local(): all_cotangents = lax.all_gather(cotangent, 'row', axis=0, tiled=True)  151 us
    psum x1, blocking collectives, local(): grad_gain = lax.psum(gain_partial, 'row')  47.4 us
    psum x1, blocking collectives, local(): grand_total = lax.psum(tile_square + leading, ('row', 'col'))  45 us
    reduce_scatter x1, waiting for transfers between devices, local(): lax.psum_scatter(partial_value.astype(jnp.bfloat16), 'col', scatter_dimen...  36 us
    dot_general x1, matrix products, local(): lax.dot_general(column_blocks, grad_blocks, (((1,), (1,)), ((0,), (0,))),...  10.9 us
    dot_general x1, matrix products, local(): lax.dot_general(all_cotangents, weights, contract_cols, preferred_element...  10.4 us
  transfers between devices with their start and end apart: 5, of which 3 were waited for; matrix products, arithmetic and copies ran while one was open for 12% of the time, Pallas kernels for 0%

commit v1 on v0

--- a/solution.py
+++ b/solution.py
@@ -80,7 +80,8 @@
     query_f = grad_wq.astype(jnp.float32)
     keyval_f = grad_wkv.astype(jnp.float32)
     tile_square = jnp.sum(query_f * query_f) + jnp.sum(keyval_f * keyval_f)
-    grad_gain = lax.psum(gain_partial, "row")
+    terms = lax.all_gather(gain_partial, "row", axis=0, tiled=False)
+    grad_gain = terms.sum(axis=0)
     leading = jnp.where(
         lax.axis_index("row") == 0, jnp.sum(grad_gain * grad_gain), jnp.float32(0.0)
     )

time: 377 us -> 389 us (1.032)
  blocking collectives: 99.7 us -> 111 us
    all_gather x0 -> x1, blocking collectives: none -> 56.9 us  [local(): terms = lax.all_gather(gain_partial, 'row', axis=0, tiled=False)]
    psum x1 -> x0, blocking collectives: 47.4 us -> none  [local(): grad_gain = lax.psum(gain_partial, 'row')]
where the time goes in v1:
time: 389 us; the launch traced here: 387 us
  waiting for transfers between devices  189 us (49%)
  blocking collectives  111 us (29%)
  other arithmetic  27.5 us (7%)
  matrix products  21.3 us (5%)
  between operations  18 us (5%)
  starting transfers between devices  11.4 us (3%)
  local copies, waits for them, and re-layouts  8.98 us (2%)
    all_gather x1, waiting for transfers between devices, local(): all_cotangents = lax.all_gather(cotangent, 'row', axis=0, tiled=True)  151 us
    all_gather x1, blocking collectives, local(): terms = lax.all_gather(gain_partial, 'row', axis=0, tiled=False)  56.9 us
    psum x1, blocking collectives, local(): grand_total = lax.psum(tile_square + leading, ('row', 'col'))  44.9 us
    reduce_scatter x1, waiting for transfers between devices, local(): lax.psum_scatter(partial_value.astype(jnp.bfloat16), 'col', scatter_dimen...  36 us
    dot_general x1, matrix products, local(): lax.dot_general(column_blocks, grad_blocks, (((1,), (1,)), ((0,), (0,))),...  10.9 us
    dot_general x1, matrix products, local(): lax.dot_general(all_cotangents, weights, contract_cols, preferred_element...  10.4 us
    psum x1, blocking collectives, local(): lax.psum(jnp.sum(weighted * input_part, axis=1, keepdims=True), 'col')  8.86 us
  transfers between devices with their start and end apart: 5, of which 3 were waited for; matrix products, arithmetic and copies ran while one was open for 12% of the time, Pallas kernels for 0%

profile of v1, /device:TPU:13, one launch (start us, length us, event | category | flops | bytes accessed | tf_op | source)
XLA Modules:
  0.0 387.1 jit_solution(4671930465909056214)
XLA Ops:
  7.2 0.0 copy-start.2
  7.2 0.0 all-gather.3.cloned.1.call-start
  7.2 2.1 pad_maximum_fusion.1
  9.3 0.0 all-gather.3.cloned.1.call-update
  9.3 0.0 copy-start
  9.3 3.3 multiply_reduce_fusion
  12.6 0.0 copy-done.2
  12.6 0.2 copy-done
  12.8 3.1 multiply_convert_fusion.1
  15.9 6.5 %copy.14 = bf16[256,8192]{0,1:T(8,128)(2,1)} copy(bf16[256,8192]{1,0:T(8,128)(2,1)} %multiply_convert_fusion.1) | data formatting | bytes 8388608 | tf_op jit(solution)/shard_map/convert_element_type | solution.py:13
  22.3 0.0 copy-start.4
  22.3 5.8 %all-to-all-start = ((bf16[256,8,1024]{0,2,1:T(8,128)(2,1)}), bf16[256,8,1024]{0,2,1:T(8,128)(2,1)}, u32[]{:S(2)}, u32[]{:S(2)}) async-start(bf16[256,8,1024]{0,2,1:T(8,128)(2,1)} %bitcast.18), calls=%async_computation.1 | async-start | bytes 8388608 | tf_op jit(solution)/shard_map/all_to_all | solution.py:64
  28.1 0.0 reduce-scatter.2.cloned.1.call-start
  28.1 150.8 %all-gather.3.cloned.1.call-done = bf16[2048,1536]{1,0:T(8,128)(2,1)} async-done(((bf16[256,1536]{1,0:T(8,128)(2,1)}), bf16[2048,1536]{1,0:T(8,128)(2,1)}) %all-gather.3.cloned.1.call-update) | async-done | bytes 6291472 | tf_op jit(solution)/shard_map/all_gather | solution.py:22
  179.0 0.0 copy-done.4
  179.0 10.4 %convolution_convert_fusion = bf16[2048,1024]{1,0:T(8,128)(2,1)} fusion(bf16[2048,1536]{1,0:T(8,128)(2,1)} %all-gather.3.cloned.1.call-done, bf16[1024,512]{1,0:T(8,128)(2,1)} %param.12, bf16[1024,1024]{1,0:T(8,128)(2,1)S(1)} %copy-done.4), kind=kOutput, calls=%fused_computation.6 | convolution fusion | flops 6450839552 | bytes 13631488 | tf_op jit(solution)/shard_map/dot_general | solution.py:24
  189.4 0.0 reduce-scatter.2.cloned.1.call-update
  189.5 6.4 %convert_element_type.33 = f32[256,8192]{1,0:T(8,128)} convert(bf16[256,8192]{1,0:T(8,128)(2,1)} %param.7) | non-fusion elementwise | flops 2097152 | bytes 12582912 | tf_op jit(solution)/shard_map/convert_element_type | solution.py:11
  195.9 0.0 all-to-all-done
  195.9 10.9 %fusion = bf16[1024,1536]{1,0:T(8,128)(2,1)S(1)} fusion(bf16[8,256,1536]{2,1,0:T(8,128)(2,1)} %bitcast.20, bf16[256,8,1024]{0,2,1:T(8,128)(2,1)} %all-to-all-done), kind=kOutput, calls=%fused_computation.3 | convolution fusion | flops 6478626816 | bytes 13631488 | tf_op jit(solution)/shard_map/dot_general | solution.py:69
  206.8 36.0 %reduce-scatter.2.cloned.1.call-done = bf16[512,1024]{1,0:T(8,128)(2,1)} async-done(((bf16[2048,1024]{1,0:T(8,128)(2,1)}), bf16[512,1024]{1,0:T(8,128)(2,1)}) %reduce-scatter.2.cloned.1.call-update) | async-done | bytes 1048592 | tf_op jit(solution)/shard_map/reduce_scatter | solution.py:27
  242.8 2.3 dynamic-slice_bitcast_fusion
  245.1 0.3 collective-permute-start.1
  245.3 5.3 %collective-permute-start = (bf16[256,1024]{1,0:T(8,128)(2,1)}, bf16[256,1024]{1,0:T(8,128)(2,1)}, u32[]{:S(2)}, u32[]{:S(2)}) collective-permute-start(bf16[256,1024]{1,0:T(8,128)(2,1)} %get-tuple-element.14), channel_id=1, source_target_pairs={{0,0},{1,8},{2,16},{3,24},{4,4},{5,12},{6,20},{7,28},{8,1},{9,9},{... | collective-permute-start | bytes 1572872 | tf_op jit(solution)/shard_map/ppermute | solution.py:42
  250.7 2.0 multiply_reduce_fusion.2
  252.7 2.9 multiply_reduce_fusion.1
  255.7 0.0 copy-start.1
  257.1 2.3 collective-permute-done.1
  259.3 0.0 collective-permute-done
  259.3 1.6 fusion.16
  260.9 2.2 fusion.12
  263.2 56.9 %all-gather = f32[16384]{0:T(1024)S(1)} all-gather(f32[2048]{0:T(1024)S(1)} %broadcast_multiply_fusion), channel_id=2, replica_groups=mesh['row'=8,'col'=4] {'row'}, dimensions={0}, use_global_device_ids=true | all-gather | bytes 73728 | tf_op jit(solution)/shard_map/all_gather | solution.py:83
  320.1 0.0 copy-start.3
  320.1 0.6 multiply_reduce_fusion.3
  321.4 8.9 %psum.14 = f32[256]{0:T(256)S(1)} all-reduce(f32[256]{0:T(256)S(1)} %get-tuple-element.6), channel_id=1, replica_groups=mesh['row'=8,'col'=4] {'col'}, use_global_device_ids=true, to_apply=%region_3.4 | all-reduce | flops 256 | bytes 2048 | tf_op jit(solution)/shard_map/psum | solution.py:56
  330.2 44.9 %psum.15 = f32[]{:T(128)} all-reduce(f32[]{:T(128)S(6)} %add.78), channel_id=1, replica_groups=mesh['row'=8,'col'=4] {'row','col'}, use_global_device_ids=true, to_apply=%region_10.11 | all-reduce | flops 1 | bytes 8 | tf_op jit(solution)/shard_map/psum | solution.py:88
  375.8 0.0 copy-done.1
  375.8 3.3 fusion.9
  379.1 0.0 copy-done.3
  (5 shorter events, 0.1 us)
Async XLA Ops:
  7.2 5.4 %copy-start.2 = (f32[8192]{0:T(1024)S(1)}, f32[8192]{0:T(1024)}, u32[]{:S(2)}) copy-start(f32[8192]{0:T(1024)} %param.8) | copy-start | bytes 98308
  7.2 171.8 %all-gather.3.cloned.1.call-start = ((), (), s32[]{:S(2)}) async-start(), calls=%async_computation.2 | async-start | bytes 7077888 | tf_op jit(solution)/shard_map/all_gather | solution.py:22
  9.3 3.5 copy-start
  22.3 156.6 %copy-start.4 = (bf16[1024,1024]{1,0:T(8,128)(2,1)S(1)}, bf16[1024,1024]{1,0:T(8,128)(2,1)}, u32[]{:S(2)}) copy-start(bf16[1024,1024]{1,0:T(8,128)(2,1)} %param.11) | copy-start | bytes 6291460
  22.3 173.5 %all-to-all-start = ((bf16[256,8,1024]{0,2,1:T(8,128)(2,1)}), bf16[256,8,1024]{0,2,1:T(8,128)(2,1)}, u32[]{:S(2)}, u32[]{:S(2)}) async-start(bf16[256,8,1024]{0,2,1:T(8,128)(2,1)} %bitcast.18), calls=%async_computation.1 | async-start | bytes 8388608 | tf_op jit(solution)/shard_map/all_to_all | solution.py:64
  28.1 214.7 %reduce-scatter.2.cloned.1.call-start = ((), (), s32[]{:S(2)}) async-start(), calls=%async_computation.3 | async-start | bytes 5242880 | tf_op jit(solution)/shard_map/reduce_scatter | solution.py:27
  245.1 14.3 %collective-permute-start.1 = (bf16[256,1024]{1,0:T(8,128)(2,1)}, bf16[256,1024]{1,0:T(8,128)(2,1)}, u32[]{:S(2)}, u32[]{:S(2)}) collective-permute-start(bf16[256,1024]{1,0:T(8,128)(2,1)} %get-tuple-element.13), channel_id=1, source_target_pairs={{0,4},{1,12},{2,20},{3,28},{4,0},{5,8},{6,16},{7,24},{8,5},{9,13},... | collective-permute-start | bytes 1572872 | tf_op jit(solution)/shard_map/ppermute | solution.py:42
  245.3 14.0 %collective-permute-start = (bf16[256,1024]{1,0:T(8,128)(2,1)}, bf16[256,1024]{1,0:T(8,128)(2,1)}, u32[]{:S(2)}, u32[]{:S(2)}) collective-permute-start(bf16[256,1024]{1,0:T(8,128)(2,1)} %get-tuple-element.14), channel_id=1, source_target_pairs={{0,0},{1,8},{2,16},{3,24},{4,4},{5,12},{6,20},{7,28},{8,1},{9,9},{... | collective-permute-start | bytes 1572872 | tf_op jit(solution)/shard_map/ppermute | solution.py:42
  255.7 120.1 %copy-start.1 = (bf16[256,2048]{1,0:T(8,128)(2,1)S(1)}, bf16[256,2048]{1,0:T(8,128)(2,1)}, u32[]{:S(2)}) copy-start(bf16[256,2048]{1,0:T(8,128)(2,1)} %param.13) | copy-start | bytes 3145732
  320.1 59.0 %copy-start.3 = (f32[2048]{0:T(1024)}, f32[2048]{0:T(1024)S(1)}, u32[]{:S(2)}) copy-start(f32[2048]{0:T(1024)S(1)} %reduce_sum.76) | copy-start | bytes 24580
Sparse Core Ops, SparseCore 0:
  10.7 168.1 all-gather.2
  189.5 53.2 reduce-scatter.1
